TPU v7x, 32 devices: a whole 2x2x4 slice. The times are simulated.
32 devices in a mesh: groups: 1, slab: 8 (over z, y), coil: 2 (over x), row: 2 (over core).
Axes of the slice: x: 2, y: 2, z: 4, core: 2. Of those that a mesh axis runs over, the one named last changes fastest.
Arguments:
- image: float32 [2, 128, 256, 128], P('groups', None, ('slab', 'row')), may hold values from -6 to 6
- sens: bfloat16 [2, 16, 128, 256, 128], P('groups', 'coil', None, ('slab', 'row')), may hold values from -1.5 to 1.5
- measured: bfloat16 [2, 16, 128, 256, 128], P('groups', 'coil', ('slab', 'row')), may hold values from -3 to 3
- mask: int32 [128, 256], P(('slab', 'row')), may hold values from 0 to 1, as said below
- thresholds: float32 [2, 7], replicated, may hold values from 0.1 to 1.5
Outputs:
- image_next: float32 [2, 128, 256, 128], P('groups', None, ('slab', 'row'))
Inputs may be any that keep to these rules, and one draw needn't show every extreme that they name: `mask`: A calibration block of the 8 central phase-encode lines (ky from 60 to 67) is sampled at every kz; outside it each (ky, kz) is sampled independently at random.
All inputs are finite; a program needn't handle non-finite values.
Results may differ from a plain program's by a relative error of at most 0.013.
Values may be sent and summed in bfloat16 or wider, within the bound.
A program may use at most 128 MiB of HBM per device.

v0:
```python
import math
import jax
import jax.numpy as jnp
from jax import lax
from jax.sharding import PartitionSpec as P

half_root = 0.7071067811865476
quarter_root = 0.3535533905932738
step_size = 0.5


def passed_along(block, axis, distance):
    devices = range(lax.axis_size(axis))
    route = [((i - distance) % len(devices), i) for i in devices]
    return lax.ppermute(block, axis, route)


def fourier_table(length, sign):
    index = jnp.arange(length, dtype=jnp.int32)
    phase = index[:, None] * index[None, :] % length
    theta = phase.astype(jnp.float32) * jnp.float32(2.0 * math.pi / length)
    scale = jnp.float32(1.0 / math.sqrt(length))
    real = jnp.cos(theta) * scale
    imaginary = jnp.sin(theta) * (sign * scale)
    upper = jnp.stack([real, -imaginary])
    lower = jnp.stack([imaginary, real])
    return jnp.stack([upper, lower]).astype(jnp.bfloat16)


def contract(form, values, table):
    return jnp.einsum(form, values, table, preferred_element_type=jnp.float32)


def complex_product(left, right):
    return jnp.stack(
        [left[0] * right[0] - left[1] * right[1], left[0] * right[1] + left[1] * right[0]]
    )


def roll_after(values, along, offset):
    return jnp.roll(values, -offset, axis=along)


def roll_before(values, along, offset):
    return jnp.roll(values, offset, axis=along)


def plane_after(values, along, offset):
    border = lax.slice_in_dim(values, 0, offset, axis=along)
    fetched = passed_along(border.astype(jnp.bfloat16), ("slab", "row"), -1).astype(border.dtype)
    remain = lax.slice_in_dim(values, offset, values.shape[along], axis=along)
    return jnp.concatenate([remain, fetched], axis=along)


def plane_before(values, along, offset):
    extent = values.shape[along]
    border = lax.slice_in_dim(values, extent - offset, extent, axis=along)
    fetched = passed_along(border.astype(jnp.bfloat16), ("slab", "row"), 1).astype(border.dtype)
    remain = lax.slice_in_dim(values, 0, extent - offset, axis=along)
    return jnp.concatenate([fetched, remain], axis=along)


def split_bands(bands, along, offset, after):
    moved = after(bands, along, offset)
    return jnp.concatenate([(bands + moved) * half_root, (bands - moved) * half_root], axis=0)


def merge_bands(bands, along, offset, before):
    half = bands.shape[0] // 2
    lower = bands[:half]
    upper = bands[half:]
    return (lower + upper + before(lower - upper, along, offset)) * quarter_root


def shrink_detail(detail, limit):
    magnitude = jnp.sqrt(detail[:, 0] * detail[:, 0] + detail[:, 1] * detail[:, 1])
    limit = limit.reshape((-1, 1, 1, 1))
    factor = jnp.maximum(magnitude - limit, 0.0) / jnp.maximum(magnitude, limit)
    return detail * factor[:, None]


def wavelet_shrink(descent, thresholds, moves):
    coarse = descent[None]
    details = []
    for level in range(thresholds.shape[0]):
        offset = 2**level
        bands = coarse
        for along, after, before in moves:
            bands = split_bands(bands, along, offset, after)
        coarse = bands[:1]
        details.append(shrink_detail(bands[1:], thresholds[level]))
    for level in reversed(range(thresholds.shape[0])):
        offset = 2**level
        bands = jnp.concatenate([coarse, details[level]], axis=0)
        for along, after, before in reversed(moves):
            bands = merge_bands(bands, along, offset, before)
        coarse = bands
    return coarse[0]


def local(image, sens, measured, mask, thresholds):
    readout_cells = image.shape[3]
    phase_cells = image.shape[1]
    depth_cells = measured.shape[3]
    table_readout = fourier_table(readout_cells, -1.0)
    table_phase = fourier_table(phase_cells, -1.0)
    table_depth = fourier_table(depth_cells, -1.0)
    inverse_readout = fourier_table(readout_cells, 1.0)
    inverse_phase = fourier_table(phase_cells, 1.0)
    inverse_depth = fourier_table(depth_cells, 1.0)
    sens_wide = sens.astype(jnp.float32)
    coil_image = complex_product(sens_wide, image[:, None]).astype(jnp.bfloat16)
    readout_done = contract("tcyzj,stjk->scyzk", coil_image, table_readout).astype(jnp.bfloat16)
    phase_done = contract("tcjzx,stjk->sckzx", readout_done, table_phase).astype(jnp.bfloat16)
    spread = lax.all_to_all(phase_done, ("slab", "row"), split_axis=2, concat_axis=3, tiled=True)
    spectrum = contract("tcyjx,stjk->scykx", spread, table_depth)
    sampled = mask.astype(jnp.float32)[None, None, :, :, None]
    residual = (sampled * (spectrum - measured.astype(jnp.float32))).astype(jnp.bfloat16)
    depth_back = contract("tcyjx,stjk->scykx", residual, inverse_depth).astype(jnp.bfloat16)
    gathered = lax.all_to_all(depth_back, ("slab", "row"), split_axis=3, concat_axis=2, tiled=True)
    phase_back = contract("tcjzx,stjk->sckzx", gathered, inverse_phase).astype(jnp.bfloat16)
    readout_back = contract("tcyzj,stjk->scyzk", phase_back, inverse_readout)
    partial_value = jnp.stack(
        [
            jnp.sum(sens_wide[0] * readout_back[0] + sens_wide[1] * readout_back[1], axis=0),
            jnp.sum(sens_wide[0] * readout_back[1] - sens_wide[1] * readout_back[0], axis=0),
        ]
    )
    gradient = lax.psum(partial_value.astype(jnp.bfloat16), "coil").astype(jnp.float32)
    descent = image - step_size * gradient
    moves = [
        (4, roll_after, roll_before),
        (2, roll_after, roll_before),
        (3, plane_after, plane_before),
    ]
    return wavelet_shrink(descent, thresholds, moves)


def solution(mesh):
    return jax.shard_map(
        local,
        mesh=mesh,
        in_specs=(
            P("groups", None, ("slab", "row"), None),
            P("groups", "coil", None, ("slab", "row"), None),
            P("groups", "coil", ("slab", "row"), None, None),
            P(("slab", "row"), None),
            P(),
        ),
        out_specs=P("groups", None, ("slab", "row"), None),
        check_vma=False,
    )
```

profile of v0, /device:TPU:0, one launch (start us, length us, event | category | flops | bytes accessed | tf_op | source)
XLA Modules:
  0.0 727.4 jit_solution(10082498368846165496)
XLA Ops:
  7.4 11.7 %copy_convert_fusion = f32[2,8,128,16,128]{4,2,0,3,1:T(8,128)} fusion(bf16[2,8,128,16,128]{4,3,2,1,0:T(8,128)(2,1)} %param.6), kind=kLoop, calls=%fused_computation.53 | loop fusion | flops 4194304 | bytes 25165824 | tf_op jit(solution)/shard_map/convert_element_type | solution.py:111
  20.0 9.9 %subtract_convert_fusion = (bf16[1,8,128,16,128]{4,2,0,3,1:T(8,128)(2,1)}, bf16[1,8,128,16,128]{4,2,0,3,1:T(8,128)(2,1)}) fusion(f32[2,8,128,16,128]{4,2,0,3,1:T(8,128)} %copy_convert_fusion, f32[128,16,128]{2,0,1:T(8,128)S(1)} %copy.36, f32[128,16,128]{2,0,1:T(8,128)S(1)} %copy.35), kind=kLoop, calls=%fused_computation.61 | loop fusion | flops 16777216 | bytes 27262976 | tf_op jit(solution)/shard_map/convert.8
  29.9 9.1 %fusion.6 = bf16[2,8,128,16,128]{4,2,3,1,0:T(8,128)(2,1)} fusion(bf16[1,8,128,16,128]{4,2,0,3,1:T(8,128)(2,1)} %get-tuple-element.8, bf16[1,8,128,16,128]{4,2,0,3,1:T(8,128)(2,1)} %get-tuple-element.7, bf16[1,2,128,128]{2,3,1,0:T(8,128)(2,1)S(1)} %get-tuple-element.28, bf16[1,2,128,128]{2,3,1,0:T(8,128)(2,1)S(1)} %get-tuple-element.29), kind=kOutput, calls=%fused_computation.30 | convolution fusion | flops 4320657408 | bytes 16908288 | tf_op jit(solution)/shard_map/tcjzx,stjk->sckzx/dot_general | solution.py:31
  39.0 12.0 %copy.38 = bf16[2,8,128,16,128]{4,3,1,0,2:T(8,128)(2,1)} copy(bf16[2,8,128,16,128]{4,2,3,1,0:T(8,128)(2,1)} %fusion.6) | data formatting | bytes 16777216 | tf_op jit(solution)/shard_map/convert_element_type | solution.py:114
  51.0 7.6 %all-to-all-start = ((bf16[2,8,128,16,128]{4,3,1,0,2:T(8,128)(2,1)}), bf16[2,8,128,16,128]{4,3,1,0,2:T(8,128)(2,1)}, u32[]{:S(2)}, u32[]{:S(2)}) async-start(bf16[2,8,128,16,128]{4,3,1,0,2:T(8,128)(2,1)} %copy.38), calls=%async_computation | async-start | bytes 16777216 | tf_op jit(solution)/shard_map/all_to_all | solution.py:115
  62.0 147.1 %all-to-all-done = bf16[2,8,128,16,128]{4,3,1,0,2:T(8,128)(2,1)} async-done(((bf16[2,8,128,16,128]{4,3,1,0,2:T(8,128)(2,1)}), bf16[2,8,128,16,128]{4,3,1,0,2:T(8,128)(2,1)}, u32[]{:S(2)}, u32[]{:S(2)}) %all-to-all-start) | async-done | bytes 8388640 | tf_op jit(solution)/shard_map/all_to_all | solution.py:115
  209.2 9.1 %copy.40 = bf16[2,8,8,16,16,128]{5,4,3,2,1,0:T(8,128)(2,1)} copy(bf16[2,8,8,16,16,128]{5,4,1,0,2,3:T(8,128)(2,1)} %bitcast.31) | data formatting | bytes 16777216 | tf_op jit(solution)/shard_map/all_to_all | solution.py:115
  218.3 9.5 %fusion.1 = bf16[2,8,8,256,128]{4,3,2,1,0:T(8,128)(2,1)S(1)} fusion(bf16[2,8,8,256,128]{4,3,2,1,0:T(8,128)(2,1)} %param.7, f32[8,256]{1,0:T(8,128)S(1)} %convert_element_type.150, bf16[2,8,8,256,128]{4,3,2,1,0:T(8,128)(2,1)} %bitcast.172, bf16[1,2,256,256]{2,3,1,0:T(8,128)(2,1)S(1)} %get-tuple-element.24, bf16[1,2,256,256]{2,3,1,0:T(8,128)(2,1)S(1)} %get-tuple-element.25), kind=kOutput, calls=%fused_computation.10 | convolution fusion | flops 4312793088 | bytes 25698304 | tf_op jit(solution)/shard_map/tcyjx,stjk->scykx/dot_general | solution.py:31
  227.9 6.7 fusion.7
  234.6 12.1 %copy.43 = bf16[2,8,8,256,128]{4,2,1,0,3:T(8,128)(2,1)} copy(bf16[2,8,8,256,128]{4,3,2,1,0:T(8,128)(2,1)} %fusion.7) | data formatting | bytes 16777216 | tf_op jit(solution)/shard_map/convert_element_type | solution.py:119
  246.6 218.8 %all_to_all.36 = bf16[2,8,8,256,128]{4,2,1,0,3:T(8,128)(2,1)} all-to-all(bf16[2,8,8,256,128]{4,2,1,0,3:T(8,128)(2,1)} %copy.43), channel_id=1, replica_groups=mesh['groups'=1,'slab'=8,'coil'=2,'row'=2] {'slab','row'}, dimensions={3} | all-to-all | bytes 16777216 | tf_op jit(solution)/shard_map/all_to_all | solution.py:120
  465.4 16.3 %copy.45 = bf16[2,8,16,8,16,128]{5,4,3,2,1,0:T(8,128)(2,1)} copy(bf16[2,8,16,8,16,128]{5,3,1,0,4,2:T(8,128)(2,1)} %bitcast.169) | data formatting | bytes 16777216 | tf_op jit(solution)/shard_map/all_to_all | solution.py:120
  481.8 12.5 %convolution_bitcast_fusion = f32[2,8,128,16,128]{4,2,0,3,1:T(8,128)} fusion(bf16[2,8,128,16,128,1]{4,3,2,1,0,5:T(8,128)(2,1)} %bitcast.168, bf16[1,2,128,128]{2,3,1,0:T(8,128)(2,1)S(1)} %get-tuple-element.30, bf16[1,2,128,128]{2,3,1,0:T(8,128)(2,1)S(1)} %get-tuple-element.27), kind=kOutput, calls=%fused_computation.29 | convolution fusion | flops 4299685888 | bytes 25296896 | tf_op jit(solution)/shard_map/tcyzj,stjk->scyzk/dot_general | solution.py:31
  494.3 13.1 %add_reduce_fusion = (bf16[128,16,128]{2,0,1:T(8,128)(2,1)S(1)}, bf16[128,16,128]{2,0,1:T(8,128)(2,1)S(1)}) fusion(f32[2,8,128,16,128]{4,2,0,3,1:T(8,128)} %convolution_bitcast_fusion, f32[2,8,128,16,128]{4,2,0,3,1:T(8,128)} %copy_convert_fusion), kind=kLoop, calls=%fused_computation.59 | loop fusion | flops 16252928 | bytes 34603008 | tf_op jit(solution)/shard_map/reduce_sum | solution.py:125
  509.1 2.0 copy.50
  511.1 39.3 %all-reduce.2.cloned.1.call-done = bf16[2,128,16,128]{1,3,2,0:T(8,128)(2,1)} async-done(((bf16[2,128,16,128]{1,3,2,0:T(8,128)(2,1)}), bf16[2,128,16,128]{1,3,2,0:T(8,128)(2,1)}) %all-reduce.2.cloned.1.call-update) | async-done | bytes 1048592 | tf_op jit(solution)/shard_map/psum | solution.py:129
  554.6 1.9 add_multiply_fusion.3
  556.6 3.6 collective-permute-start
  560.1 3.8 fusion.22
  564.1 6.8 subtract_multiply_fusion
  571.7 3.0 fusion.41
  574.7 4.0 fusion.40
  578.7 4.2 subtract_multiply_fusion.2
  583.0 4.7 collective-permute-start.1
  587.7 5.4 divide_bitcast_fusion
  593.1 3.1 fusion.23
  596.3 8.9 %subtract_multiply_fusion.1 = (f32[4,2,128,16,128]{2,4,3,1,0:T(8,128)}, f32[4,2,128,16,128]{2,4,3,1,0:T(8,128)S(1)}) fusion(f32[4,2,128,2,128]{2,4,3,1,0:T(8,128)S(1)} %convert_element_type.163, f32[4,2,128,14,128]{2,4,3,1,0:T(8,128)} %fusion.23, f32[2,2,128,16,128]{2,4,3,1,0:T(8,128)} %copy-done.4, f32[2,2,128,16,128]{2,4,3,1,0:T(8,128)} %copy-done.5), kind=kLoop, calls=%fused_computation.55 | loop fusion | flops 12582912 | bytes 33554432 | tf_op jit(solution)/shard_map/mul | solution.py:65
  605.5 3.0 copy-done.1
  608.4 7.7 %divide_bitcast_fusion.1 = f32[7,128,16,128]{1,3,2,0:T(8,128)} fusion(f32[4,2,128,16,128]{2,4,3,1,0:T(8,128)} %get-tuple-element.9, f32[4,2,128,16,128]{2,4,3,1,0:T(8,128)S(1)} %get-tuple-element.10, f32[7]{0:T(128)S(1)} %get-tuple-element.31), kind=kLoop, calls=%fused_computation.79 | loop fusion | flops 16515072 | bytes 24117276 | tf_op jit(solution)/shard_map/mul | solution.py:79
  616.2 8.2 %fusion.5 = f32[7,2,128,16,128]{2,4,3,1,0:T(8,128)S(1)} fusion(f32[4,2,128,16,128]{2,4,3,1,0:T(8,128)} %copy-done.1, f32[4,2,128,16,128]{2,4,3,1,0:T(8,128)} %get-tuple-element.9, f32[7,128,16,128]{1,3,2,0:T(8,128)} %divide_bitcast_fusion.1), kind=kLoop, calls=%fused_computation.18 | loop fusion | flops 7340032 | bytes 38797312 | tf_op jit(solution)/shard_map/mul | solution.py:79
  624.4 4.0 slice_subtract_fusion.1
  629.8 11.4 %fusion.3 = f32[7,2,128,16,128]{2,4,3,1,0:T(8,128)} fusion(f32[4,2,128,16,128]{2,4,3,1,0:T(8,128)S(1)} %bitcast.165, f32[4,2,128,16,128]{2,4,3,1,0:T(8,128)} %copy-done.3, f32[7,128,16,128]{1,3,2,0:T(8,128)} %divide_bitcast_fusion), kind=kLoop, calls=%fused_computation.16 | loop fusion | flops 7340032 | bytes 38797312 | tf_op jit(solution)/shard_map/mul | solution.py:79
  641.3 6.9 slice.282
  648.3 6.9 fusion.10
  655.2 4.2 slice_subtract_fusion.3
  659.4 3.2 slice.285
  662.7 9.9 %fusion.44 = f32[2,2,128,16,128]{2,4,3,1,0:T(8,128)} fusion(f32[2,2,126,16,128]{2,4,3,1,0:T(8,128)} %bitcast.166, f32[2,2,2,16,128]{2,4,3,1,0:T(8,128)} %slice.285, f32[4,2,128,16,128]{2,4,3,1,0:T(8,128)} %fusion.10), kind=kLoop, calls=%fused_computation.97 | loop fusion | flops 4194304 | bytes 16777216 | tf_op jit(solution)/shard_map/mul | solution.py:72
  672.6 2.6 slice_subtract_fusion.5
  675.3 2.9 fusion.50
  678.2 1.8 slice_subtract_fusion
  680.1 3.3 copy-done.10
  683.5 7.3 %slice.297 = f32[4,2,128,15,128]{2,4,3,1,0:T(8,128)} slice(f32[4,2,128,16,128]{2,4,3,1,0:T(8,128)} %copy-done.10), slice={[0:4], [0:2], [0:128], [0:15], [0:128]} | slice | bytes 15728640 | tf_op jit(solution)/shard_map/slice | solution.py:59
  692.0 7.2 fusion.11
  699.2 4.2 slice_subtract_fusion.2
  703.4 3.3 slice.300
  708.3 5.7 fusion.45
  714.0 2.6 slice_subtract_fusion.4
  718.3 2.0 copy.52
  (87 shorter events, 18.3 us)
Async XLA Ops:
  7.4 11.7 %copy-start.11 = (f32[2,128,16,128]{3,2,1,0:T(8,128)S(1)}, f32[2,128,16,128]{3,2,1,0:T(8,128)}, u32[]{:S(2)}) copy-start(f32[2,128,16,128]{3,2,1,0:T(8,128)} %param.5) | copy-start | bytes 6291460
  51.0 7.7 %copy-start.13 = (s32[8,256]{1,0:T(8,128)S(1)}, s32[8,256]{1,0:T(8,128)}, u32[]{:S(2)}) copy-start(s32[8,256]{1,0:T(8,128)} %param.8) | copy-start | bytes 24580
  51.0 158.2 %all-to-all-start = ((bf16[2,8,128,16,128]{4,3,1,0,2:T(8,128)(2,1)}), bf16[2,8,128,16,128]{4,3,1,0,2:T(8,128)(2,1)}, u32[]{:S(2)}, u32[]{:S(2)}) async-start(bf16[2,8,128,16,128]{4,3,1,0,2:T(8,128)(2,1)} %copy.38), calls=%async_computation | async-start | bytes 16777216 | tf_op jit(solution)/shard_map/all_to_all | solution.py:115
  58.6 491.8 %all-reduce.2.cloned.1.call-start = ((), (), s32[]{:S(2)}) async-start(), calls=%async_computation.2 | async-start | bytes 2097152 | tf_op jit(solution)/shard_map/psum | solution.py:129
  507.4 3.7 copy-start.14
  550.4 1.9 copy-start.12
  556.5 7.4 %copy-start.6 = (f32[2,2,128,16,128]{2,4,3,1,0:T(8,128)}, f32[2,2,128,16,128]{2,4,3,1,0:T(8,128)S(1)}, u32[]{:S(2)}) copy-start(f32[2,2,128,16,128]{2,4,3,1,0:T(8,128)S(1)} %get-tuple-element.15) | copy-start | bytes 12582916
  556.5 7.4 %copy-start.7 = (f32[2,2,128,16,128]{2,4,3,1,0:T(8,128)}, f32[2,2,128,16,128]{2,4,3,1,0:T(8,128)S(1)}, u32[]{:S(2)}) copy-start(f32[2,2,128,16,128]{2,4,3,1,0:T(8,128)S(1)} %get-tuple-element.16) | copy-start | bytes 12582916
  556.6 7.5 %collective-permute-start = (bf16[4,2,128,1,128]{2,4,3,1,0:T(8,128)(2,1)S(1)}, bf16[4,2,128,1,128]{2,4,3,1,0:T(8,128)(2,1)S(1)}, u32[]{:S(2)}, u32[]{:S(2)}) collective-permute-start(bf16[4,2,128,1,128]{2,4,3,1,0:T(8,128)(2,1)S(1)} %fusion.61), channel_id=1, source_target_pairs={{1,0},{4,1},{5,4},{8,5},{9,8},{12,9},{13,12},{16,13},{17,16},{20,1... | collective-permute-start | bytes 786440 | tf_op jit(solution)/shard_map/ppermute | solution.py:15
  570.9 16.8 %copy-start = (f32[4,2,128,16,128]{2,4,3,1,0:T(8,128)}, f32[4,2,128,16,128]{2,4,3,1,0:T(8,128)S(1)}, u32[]{:S(2)}) copy-start(f32[4,2,128,16,128]{2,4,3,1,0:T(8,128)S(1)} %get-tuple-element.12) | copy-start | bytes 25165828
  570.9 16.8 %copy-start.3 = (f32[4,2,128,16,128]{2,4,3,1,0:T(8,128)}, f32[4,2,128,16,128]{2,4,3,1,0:T(8,128)S(1)}, u32[]{:S(2)}) copy-start(f32[4,2,128,16,128]{2,4,3,1,0:T(8,128)S(1)} %get-tuple-element.11) | copy-start | bytes 25165828
  582.9 10.1 %copy-start.4 = (f32[2,2,128,16,128]{2,4,3,1,0:T(8,128)}, f32[2,2,128,16,128]{2,4,3,1,0:T(8,128)S(1)}, u32[]{:S(2)}) copy-start(f32[2,2,128,16,128]{2,4,3,1,0:T(8,128)S(1)} %get-tuple-element.13) | copy-start | bytes 12582916
  582.9 10.1 %copy-start.5 = (f32[2,2,128,16,128]{2,4,3,1,0:T(8,128)}, f32[2,2,128,16,128]{2,4,3,1,0:T(8,128)S(1)}, u32[]{:S(2)}) copy-start(f32[2,2,128,16,128]{2,4,3,1,0:T(8,128)S(1)} %get-tuple-element.14) | copy-start | bytes 12582916
  583.0 13.2 %collective-permute-start.1 = (bf16[4,2,128,2,128]{2,4,3,1,0:T(8,128)(2,1)S(1)}, bf16[4,2,128,2,128]{2,4,3,1,0:T(8,128)(2,1)S(1)}, u32[]{:S(2)}, u32[]{:S(2)}) collective-permute-start(bf16[4,2,128,2,128]{2,4,3,1,0:T(8,128)(2,1)S(1)} %fusion.54), channel_id=1, source_target_pairs={{1,0},{4,1},{5,4},{8,5},{9,8},{12,9},{13,12},{16,13},{17,16},{20,1... | collective-permute-start | bytes 1572872 | tf_op jit(solution)/shard_map/ppermute | solution.py:15
  605.2 3.2 copy-start.1
  608.4 21.4 %slice-start.4 = ((s8[8388608]{0:T(1024)(128)(4,1)}), s8[4194304]{0:T(1024)(128)(4,1)S(1)}, s32[]{:S(2)}) async-start(s8[8388608]{0:T(1024)(128)(4,1)} %bitcast.164), calls=%async_computation.7 | async-start | bytes 8388608
  616.2 13.6 %slice-start.5 = ((s8[8388608]{0:T(1024)(128)(4,1)}), s8[4194304]{0:T(1024)(128)(4,1)S(1)}, s32[]{:S(2)}) async-start(s8[8388608]{0:T(1024)(128)(4,1)} %bitcast.164), calls=%async_computation.8 | async-start | bytes 8388608
  629.7 18.5 %collective-permute-start.2 = (bf16[4,2,128,2,128]{2,4,3,1,0:T(8,128)(2,1)S(1)}, bf16[4,2,128,2,128]{2,4,3,1,0:T(8,128)(2,1)S(1)}, u32[]{:S(2)}, u32[]{:S(2)}) collective-permute-start(bf16[4,2,128,2,128]{2,4,3,1,0:T(8,128)(2,1)S(1)} %slice.450), channel_id=1, source_target_pairs={{29,0},{0,1},{1,4},{4,5},{5,8},{8,9},{9,12},{12,13},{13,16},{16,17... | collective-permute-start | bytes 1572872 | tf_op jit(solution)/shard_map/ppermute | solution.py:15
  659.4 3.2 copy-start.8
  662.7 15.5 %slice-start = ((s8[14680064]{0:T(1024)(128)(4,1)}), s8[4194304]{0:T(1024)(128)(4,1)S(1)}, s32[]{:S(2)}) async-start(s8[14680064]{0:T(1024)(128)(4,1)} %bitcast.162), calls=%async_computation.3 | async-start | bytes 8388608
  662.7 15.5 %slice-start.1 = ((s8[14680064]{0:T(1024)(128)(4,1)}), s8[4194304]{0:T(1024)(128)(4,1)S(1)}, s32[]{:S(2)}) async-start(s8[14680064]{0:T(1024)(128)(4,1)} %bitcast.162), calls=%async_computation.4 | async-start | bytes 8388608
  662.7 15.6 %slice-start.2 = ((s8[14680064]{0:T(1024)(128)(4,1)}), s8[2097152]{0:T(1024)(128)(4,1)S(1)}, s32[]{:S(2)}) async-start(s8[14680064]{0:T(1024)(128)(4,1)} %bitcast.162), calls=%async_computation.5 | async-start | bytes 4194304
  672.6 5.6 slice-start.3
  680.1 3.3 copy-start.10
  683.4 8.5 %collective-permute-start.3 = (bf16[4,2,128,1,128]{2,4,3,1,0:T(8,128)(2,1)S(1)}, bf16[4,2,128,1,128]{2,4,3,1,0:T(8,128)(2,1)S(1)}, u32[]{:S(2)}, u32[]{:S(2)}) collective-permute-start(bf16[4,2,128,1,128]{2,4,3,1,0:T(8,128)(2,1)S(1)} %slice.451), channel_id=1, source_target_pairs={{29,0},{0,1},{1,4},{4,5},{5,8},{8,9},{9,12},{12,13},{13,16},{16,17... | collective-permute-start | bytes 786440 | tf_op jit(solution)/shard_map/ppermute | solution.py:15
  703.4 4.9 copy-start.2
  714.0 3.4 copy-start.9
Sparse Core Ops, SparseCore 0:
  509.2 41.1 all-reduce.1
where the time goes:
time: 731 us; the launch traced here: 727 us
  blocking collectives  219 us (30%)
  waiting for transfers between devices  188 us (26%)
  other arithmetic  166 us (23%)
  local copies, waits for them, and re-layouts  86.6 us (12%)
  matrix products  37.9 us (5%)
  starting transfers between devices  16 us (2%)
  between operations  14.2 us (2%)
    all_to_all x1, blocking collectives, local(): lax.all_to_all(depth_back, ('slab', 'row'), split_axis=3, concat_axis=2,...  219 us
    all_to_all x1, waiting for transfers between devices, local(): lax.all_to_all(phase_done, ('slab', 'row'), split_axis=2, concat_axis=3,...  147 us
    psum x1, waiting for transfers between devices, local(): lax.psum(partial_value.astype(jnp.bfloat16), 'coil').astype(jnp.float32)  39.3 us
    dot_general x4, matrix products, contract(): return jnp.einsum(form, values, table, preferred_element_type=jnp.float32)  37.9 us
    mul x4, other arithmetic, shrink_detail(): return detail * factor[:, None]  32.8 us
    mul x5, other arithmetic, merge_bands(): return (lower + upper + before(lower - upper, along, offset)) * quarter_root  32.6 us
    mul x3, other arithmetic, split_bands(): (bands - moved) * half_root  19.9 us
    sub x6, other arithmetic, merge_bands(): return (lower + upper + before(lower - upper, along, offset)) * quarter_root  19.6 us
  transfers between devices with their start and end apart: 6, of which 4 were waited for; matrix products, arithmetic and copies ran while one was open for 6% of the time, Pallas kernels for 0%

commit v1 on v0

--- a/solution.py
+++ b/solution.py
@@ -112,7 +112,15 @@
     coil_image = complex_product(sens_wide, image[:, None]).astype(jnp.bfloat16)
     readout_done = contract("tcyzj,stjk->scyzk", coil_image, table_readout).astype(jnp.bfloat16)
     phase_done = contract("tcjzx,stjk->sckzx", readout_done, table_phase).astype(jnp.bfloat16)
-    spread = lax.all_to_all(phase_done, ("slab", "row"), split_axis=2, concat_axis=3, tiled=True)
+    spread = jnp.concatenate(
+        lax.all_to_all(
+            jnp.stack(jnp.split(phase_done, lax.axis_size(("slab", "row")), axis=2)),
+            ("slab", "row"),
+            0,
+            0,
+        ),
+        axis=3,
+    )
     spectrum = contract("tcyjx,stjk->scykx", spread, table_depth)
     sampled = mask.astype(jnp.float32)[None, None, :, :, None]
     residual = (sampled * (spectrum - measured.astype(jnp.float32))).astype(jnp.bfloat16)

time: 731 us -> 753 us (1.030)
  local copies, waits for them, and re-layouts: 86.6 us -> 105 us
    unnamed x45 -> x60, local copies, waits for them, and re-layouts: 11.3 us -> 39.7 us
    convert_element_type x1 -> x0, local copies, waits for them, and re-layouts: 12 us -> none  [local(): contract('tcjzx,stjk->sckzx', readout_done, table_phase)]
    all_to_all x1 -> x0, local copies, waits for them, and re-layouts: 9.14 us -> none  [local(): lax.all_to_all(phase_done, ('slab', 'row'), split_axis=2, concat_axis=3,...]
    reshape x0 -> x1, local copies, waits for them, and re-layouts: none -> 9.09 us  [local(): jnp.concatenate(lax.all_to_all(jnp.stack(jnp.split(phase_done, lax.axis_s...]
  transfers between devices with their start and end apart: 6 -> 6, of which waited for: 4 -> 3; matrix products, arithmetic and copies ran while one was open for 6% -> 6% of each run, Pallas kernels for 0% -> 0%
where the time goes in v1:
time: 753 us; the launch traced here: 745 us
  blocking collectives  219 us (29%)
  waiting for transfers between devices  187 us (25%)
  other arithmetic  166 us (22%)
  local copies, waits for them, and re-layouts  105 us (14%)
  matrix products  38.2 us (5%)
  starting transfers between devices  16.1 us (2%)
  between operations  14.2 us (2%)
    all_to_all x1, blocking collectives, local(): lax.all_to_all(depth_back, ('slab', 'row'), split_axis=3, concat_axis=2,...  219 us
    all_to_all x1, waiting for transfers between devices, local(): lax.all_to_all(jnp.stack(jnp.split(phase_done, lax.axis_size(('slab', 'ro...  147 us
    unnamed x60, local copies, waits for them, and re-layouts  39.7 us
    psum x1, waiting for transfers between devices, local(): lax.psum(partial_value.astype(jnp.bfloat16), 'coil').astype(jnp.float32)  39.3 us
    dot_general x4, matrix products, contract(): return jnp.einsum(form, values, table, preferred_element_type=jnp.float32)  38.2 us
    mul x4, other arithmetic, shrink_detail(): return detail * factor[:, None]  32.7 us
    mul x5, other arithmetic, merge_bands(): return (lower + upper + before(lower - upper, along, offset)) * quarter_root  32.6 us
    mul x3, other arithmetic, split_bands(): (bands - moved) * half_root  19.9 us
  transfers between devices with their start and end apart: 6, of which 3 were waited for; matrix products, arithmetic and copies ran while one was open for 6% of the time, Pallas kernels for 0%

profile of v1, /device:TPU:0, one launch (start us, length us, event | category | flops | bytes accessed | tf_op | source)
XLA Modules:
  0.0 745.3 jit_solution(6939945134582914592)
XLA Ops:
  7.4 11.7 %copy_convert_fusion = f32[2,8,128,16,128]{4,2,0,3,1:T(8,128)} fusion(bf16[2,8,128,16,128]{4,3,2,1,0:T(8,128)(2,1)} %param.6), kind=kLoop, calls=%fused_computation.53 | loop fusion | flops 4194304 | bytes 25165824 | tf_op jit(solution)/shard_map/convert_element_type | solution.py:111
  20.0 9.4 %subtract_convert_fusion = (bf16[1,8,128,16,128]{4,2,0,3,1:T(8,128)(2,1)}, bf16[1,8,128,16,128]{4,2,0,3,1:T(8,128)(2,1)}) fusion(f32[2,8,128,16,128]{4,2,0,3,1:T(8,128)} %copy_convert_fusion, f32[128,16,128]{2,0,1:T(8,128)S(1)} %copy.36, f32[128,16,128]{2,0,1:T(8,128)S(1)} %copy.35), kind=kLoop, calls=%fused_computation.61 | loop fusion | flops 16777216 | bytes 27262976 | tf_op jit(solution)/shard_map/convert.8
  29.4 9.1 %fusion.6 = bf16[2,8,128,16,128]{4,2,3,1,0:T(8,128)(2,1)} fusion(bf16[1,8,128,16,128]{4,2,0,3,1:T(8,128)(2,1)} %get-tuple-element.8, bf16[1,8,128,16,128]{4,2,0,3,1:T(8,128)(2,1)} %get-tuple-element.7, bf16[1,2,128,128]{2,3,1,0:T(8,128)(2,1)S(1)} %get-tuple-element.28, bf16[1,2,128,128]{2,3,1,0:T(8,128)(2,1)S(1)} %get-tuple-element.29), kind=kOutput, calls=%fused_computation.30 | convolution fusion | flops 4320657408 | bytes 16908288 | tf_op jit(solution)/shard_map/tcjzx,stjk->sckzx/dot_general | solution.py:31
  38.4 1.9 fusion.72
  63.1 1.9 fusion.59
  68.8 7.6 %all-to-all-start = ((bf16[16,2,8,8,16,128]{5,3,4,2,1,0:T(8,128)(2,1)}), bf16[16,2,8,8,16,128]{5,3,4,2,1,0:T(8,128)(2,1)}, u32[]{:S(2)}, u32[]{:S(2)}) async-start(bf16[16,2,8,8,16,128]{5,3,4,2,1,0:T(8,128)(2,1)} %fusion.57), calls=%async_computation | async-start | bytes 16777216 | tf_op jit(solution)/shard_map/all_to_all | solution.py:116
  80.0 147.0 %all-to-all-done = bf16[16,2,8,8,16,128]{5,3,4,2,1,0:T(8,128)(2,1)} async-done(((bf16[16,2,8,8,16,128]{5,3,4,2,1,0:T(8,128)(2,1)}), bf16[16,2,8,8,16,128]{5,3,4,2,1,0:T(8,128)(2,1)}, u32[]{:S(2)}, u32[]{:S(2)}) %all-to-all-start) | async-done | bytes 8388640 | tf_op jit(solution)/shard_map/all_to_all | solution.py:116
  227.0 9.1 %copy.38 = bf16[2,8,8,16,16,128]{5,4,3,2,1,0:T(8,128)(2,1)} copy(bf16[2,8,8,16,16,128]{5,2,4,1,0,3:T(8,128)(2,1)} %bitcast.45) | data formatting | bytes 16777216 | tf_op jit(solution)/shard_map/reshape | solution.py:115
  236.1 9.5 %fusion.1 = bf16[2,8,8,256,128]{4,3,2,1,0:T(8,128)(2,1)S(1)} fusion(bf16[2,8,8,256,128]{4,3,2,1,0:T(8,128)(2,1)} %param.7, f32[8,256]{1,0:T(8,128)S(1)} %convert_element_type.150, bf16[2,8,8,256,128]{4,3,2,1,0:T(8,128)(2,1)} %bitcast.234, bf16[1,2,256,256]{2,3,1,0:T(8,128)(2,1)S(1)} %get-tuple-element.24, bf16[1,2,256,256]{2,3,1,0:T(8,128)(2,1)S(1)} %get-tuple-element.25), kind=kOutput, calls=%fused_computation.10 | convolution fusion | flops 4312793088 | bytes 25698304 | tf_op jit(solution)/shard_map/tcyjx,stjk->scykx/dot_general | solution.py:31
  245.6 7.2 fusion.7
  252.8 12.1 %copy.41 = bf16[2,8,8,256,128]{4,2,1,0,3:T(8,128)(2,1)} copy(bf16[2,8,8,256,128]{4,3,2,1,0:T(8,128)(2,1)} %fusion.7) | data formatting | bytes 16777216 | tf_op jit(solution)/shard_map/convert_element_type | solution.py:127
  264.9 218.8 %all_to_all.23 = bf16[2,8,8,256,128]{4,2,1,0,3:T(8,128)(2,1)} all-to-all(bf16[2,8,8,256,128]{4,2,1,0,3:T(8,128)(2,1)} %copy.41), channel_id=1, replica_groups=mesh['groups'=1,'slab'=8,'coil'=2,'row'=2] {'slab','row'}, dimensions={3} | all-to-all | bytes 16777216 | tf_op jit(solution)/shard_map/all_to_all | solution.py:128
  483.6 16.3 %copy.43 = bf16[2,8,16,8,16,128]{5,4,3,2,1,0:T(8,128)(2,1)} copy(bf16[2,8,16,8,16,128]{5,3,1,0,4,2:T(8,128)(2,1)} %bitcast.231) | data formatting | bytes 16777216 | tf_op jit(solution)/shard_map/all_to_all | solution.py:128
  500.0 12.3 %convolution_bitcast_fusion = f32[2,8,128,16,128]{4,2,0,3,1:T(8,128)} fusion(bf16[2,8,128,16,128,1]{4,3,2,1,0,5:T(8,128)(2,1)} %bitcast.230, bf16[1,2,128,128]{2,3,1,0:T(8,128)(2,1)S(1)} %get-tuple-element.30, bf16[1,2,128,128]{2,3,1,0:T(8,128)(2,1)S(1)} %get-tuple-element.27), kind=kOutput, calls=%fused_computation.29 | convolution fusion | flops 4299685888 | bytes 25296896 | tf_op jit(solution)/shard_map/tcyzj,stjk->scyzk/dot_general | solution.py:31
  512.3 13.1 %add_reduce_fusion = (bf16[128,16,128]{2,0,1:T(8,128)(2,1)S(1)}, bf16[128,16,128]{2,0,1:T(8,128)(2,1)S(1)}) fusion(f32[2,8,128,16,128]{4,2,0,3,1:T(8,128)} %convolution_bitcast_fusion, f32[2,8,128,16,128]{4,2,0,3,1:T(8,128)} %copy_convert_fusion), kind=kLoop, calls=%fused_computation.59 | loop fusion | flops 16252928 | bytes 34603008 | tf_op jit(solution)/shard_map/reduce_sum | solution.py:133
  527.1 2.0 copy.48
  529.1 39.3 %all-reduce.2.cloned.1.call-done = bf16[2,128,16,128]{1,3,2,0:T(8,128)(2,1)} async-done(((bf16[2,128,16,128]{1,3,2,0:T(8,128)(2,1)}), bf16[2,128,16,128]{1,3,2,0:T(8,128)(2,1)}) %all-reduce.2.cloned.1.call-update) | async-done | bytes 1048592 | tf_op jit(solution)/shard_map/psum | solution.py:137
  572.6 1.9 add_multiply_fusion.3
  574.6 3.6 collective-permute-start
  578.2 4.0 fusion.22
  582.2 6.8 subtract_multiply_fusion
  589.9 3.0 fusion.41
  592.9 4.0 fusion.40
  596.9 4.2 subtract_multiply_fusion.2
  601.2 4.5 collective-permute-start.1
  605.7 5.4 divide_bitcast_fusion
  611.1 3.1 fusion.23
  614.4 8.9 %subtract_multiply_fusion.1 = (f32[4,2,128,16,128]{2,4,3,1,0:T(8,128)}, f32[4,2,128,16,128]{2,4,3,1,0:T(8,128)S(1)}) fusion(f32[4,2,128,2,128]{2,4,3,1,0:T(8,128)S(1)} %convert_element_type.163, f32[4,2,128,14,128]{2,4,3,1,0:T(8,128)} %fusion.23, f32[2,2,128,16,128]{2,4,3,1,0:T(8,128)} %copy-done.4, f32[2,2,128,16,128]{2,4,3,1,0:T(8,128)} %copy-done.5), kind=kLoop, calls=%fused_computation.55 | loop fusion | flops 12582912 | bytes 33554432 | tf_op jit(solution)/shard_map/mul | solution.py:65
  623.5 3.0 copy-done.1
  626.5 7.7 %divide_bitcast_fusion.1 = f32[7,128,16,128]{1,3,2,0:T(8,128)} fusion(f32[4,2,128,16,128]{2,4,3,1,0:T(8,128)} %get-tuple-element.9, f32[4,2,128,16,128]{2,4,3,1,0:T(8,128)S(1)} %get-tuple-element.10, f32[7]{0:T(128)S(1)} %get-tuple-element.31), kind=kLoop, calls=%fused_computation.79 | loop fusion | flops 16515072 | bytes 24117276 | tf_op jit(solution)/shard_map/mul | solution.py:79
  634.2 8.2 %fusion.5 = f32[7,2,128,16,128]{2,4,3,1,0:T(8,128)S(1)} fusion(f32[4,2,128,16,128]{2,4,3,1,0:T(8,128)} %copy-done.1, f32[4,2,128,16,128]{2,4,3,1,0:T(8,128)} %get-tuple-element.9, f32[7,128,16,128]{1,3,2,0:T(8,128)} %divide_bitcast_fusion.1), kind=kLoop, calls=%fused_computation.18 | loop fusion | flops 7340032 | bytes 38797312 | tf_op jit(solution)/shard_map/mul | solution.py:79
  642.4 4.0 slice_subtract_fusion.1
  647.9 11.4 %fusion.3 = f32[7,2,128,16,128]{2,4,3,1,0:T(8,128)} fusion(f32[4,2,128,16,128]{2,4,3,1,0:T(8,128)S(1)} %bitcast.227, f32[4,2,128,16,128]{2,4,3,1,0:T(8,128)} %copy-done.3, f32[7,128,16,128]{1,3,2,0:T(8,128)} %divide_bitcast_fusion), kind=kLoop, calls=%fused_computation.16 | loop fusion | flops 7340032 | bytes 38797312 | tf_op jit(solution)/shard_map/mul | solution.py:79
  659.3 6.9 slice.282
  666.3 6.9 fusion.10
  673.2 4.2 slice_subtract_fusion.3
  677.4 3.2 slice.285
  680.7 9.9 %fusion.44 = f32[2,2,128,16,128]{2,4,3,1,0:T(8,128)} fusion(f32[2,2,126,16,128]{2,4,3,1,0:T(8,128)} %bitcast.228, f32[2,2,2,16,128]{2,4,3,1,0:T(8,128)} %slice.285, f32[4,2,128,16,128]{2,4,3,1,0:T(8,128)} %fusion.10), kind=kLoop, calls=%fused_computation.97 | loop fusion | flops 4194304 | bytes 16777216 | tf_op jit(solution)/shard_map/mul | solution.py:72
  690.6 2.6 slice_subtract_fusion.5
  693.2 2.9 fusion.50
  698.1 3.3 copy-done.10
  701.5 7.3 slice.297
  710.0 7.2 fusion.11
  717.2 4.2 slice_subtract_fusion.2
  721.4 3.3 slice.300
  726.3 5.7 fusion.45
  732.0 2.6 slice_subtract_fusion.4
  736.3 2.0 copy.50
  (102 shorter events, 46.7 us)
Async XLA Ops:
  7.4 11.7 %copy-start.11 = (f32[2,128,16,128]{3,2,1,0:T(8,128)S(1)}, f32[2,128,16,128]{3,2,1,0:T(8,128)}, u32[]{:S(2)}) copy-start(f32[2,128,16,128]{3,2,1,0:T(8,128)} %param.5) | copy-start | bytes 6291460
  68.8 8.0 %copy-start.13 = (s32[8,256]{1,0:T(8,128)S(1)}, s32[8,256]{1,0:T(8,128)}, u32[]{:S(2)}) copy-start(s32[8,256]{1,0:T(8,128)} %param.8) | copy-start | bytes 24580
  68.8 158.2 %all-to-all-start = ((bf16[16,2,8,8,16,128]{5,3,4,2,1,0:T(8,128)(2,1)}), bf16[16,2,8,8,16,128]{5,3,4,2,1,0:T(8,128)(2,1)}, u32[]{:S(2)}, u32[]{:S(2)}) async-start(bf16[16,2,8,8,16,128]{5,3,4,2,1,0:T(8,128)(2,1)} %fusion.57), calls=%async_computation | async-start | bytes 16777216 | tf_op jit(solution)/shard_map/all_to_all | solution.py:116
  76.4 492.0 %all-reduce.2.cloned.1.call-start = ((), (), s32[]{:S(2)}) async-start(), calls=%async_computation.2 | async-start | bytes 2097152 | tf_op jit(solution)/shard_map/psum | solution.py:137
  525.4 3.7 copy-start.14
  568.4 1.9 copy-start.12
  574.5 7.6 %copy-start.6 = (f32[2,2,128,16,128]{2,4,3,1,0:T(8,128)}, f32[2,2,128,16,128]{2,4,3,1,0:T(8,128)S(1)}, u32[]{:S(2)}) copy-start(f32[2,2,128,16,128]{2,4,3,1,0:T(8,128)S(1)} %get-tuple-element.15) | copy-start | bytes 12582916
  574.6 7.6 %copy-start.7 = (f32[2,2,128,16,128]{2,4,3,1,0:T(8,128)}, f32[2,2,128,16,128]{2,4,3,1,0:T(8,128)S(1)}, u32[]{:S(2)}) copy-start(f32[2,2,128,16,128]{2,4,3,1,0:T(8,128)S(1)} %get-tuple-element.16) | copy-start | bytes 12582916
  574.6 7.6 %collective-permute-start = (bf16[4,2,128,1,128]{2,4,3,1,0:T(8,128)(2,1)S(1)}, bf16[4,2,128,1,128]{2,4,3,1,0:T(8,128)(2,1)S(1)}, u32[]{:S(2)}, u32[]{:S(2)}) collective-permute-start(bf16[4,2,128,1,128]{2,4,3,1,0:T(8,128)(2,1)S(1)} %fusion.77), channel_id=1, source_target_pairs={{1,0},{4,1},{5,4},{8,5},{9,8},{12,9},{13,12},{16,13},{17,16},{20,1... | collective-permute-start | bytes 786440 | tf_op jit(solution)/shard_map/ppermute | solution.py:15
  589.0 16.7 %copy-start = (f32[4,2,128,16,128]{2,4,3,1,0:T(8,128)}, f32[4,2,128,16,128]{2,4,3,1,0:T(8,128)S(1)}, u32[]{:S(2)}) copy-start(f32[4,2,128,16,128]{2,4,3,1,0:T(8,128)S(1)} %get-tuple-element.12) | copy-start | bytes 25165828
  589.1 16.6 %copy-start.3 = (f32[4,2,128,16,128]{2,4,3,1,0:T(8,128)}, f32[4,2,128,16,128]{2,4,3,1,0:T(8,128)S(1)}, u32[]{:S(2)}) copy-start(f32[4,2,128,16,128]{2,4,3,1,0:T(8,128)S(1)} %get-tuple-element.11) | copy-start | bytes 25165828
  601.1 10.0 %copy-start.4 = (f32[2,2,128,16,128]{2,4,3,1,0:T(8,128)}, f32[2,2,128,16,128]{2,4,3,1,0:T(8,128)S(1)}, u32[]{:S(2)}) copy-start(f32[2,2,128,16,128]{2,4,3,1,0:T(8,128)S(1)} %get-tuple-element.13) | copy-start | bytes 12582916
  601.1 10.0 %copy-start.5 = (f32[2,2,128,16,128]{2,4,3,1,0:T(8,128)}, f32[2,2,128,16,128]{2,4,3,1,0:T(8,128)S(1)}, u32[]{:S(2)}) copy-start(f32[2,2,128,16,128]{2,4,3,1,0:T(8,128)S(1)} %get-tuple-element.14) | copy-start | bytes 12582916
  601.2 13.1 %collective-permute-start.1 = (bf16[4,2,128,2,128]{2,4,3,1,0:T(8,128)(2,1)S(1)}, bf16[4,2,128,2,128]{2,4,3,1,0:T(8,128)(2,1)S(1)}, u32[]{:S(2)}, u32[]{:S(2)}) collective-permute-start(bf16[4,2,128,2,128]{2,4,3,1,0:T(8,128)(2,1)S(1)} %fusion.54), channel_id=1, source_target_pairs={{1,0},{4,1},{5,4},{8,5},{9,8},{12,9},{13,12},{16,13},{17,16},{20,1... | collective-permute-start | bytes 1572872 | tf_op jit(solution)/shard_map/ppermute | solution.py:15
  623.3 3.2 copy-start.1
  626.5 21.4 %slice-start.4 = ((s8[8388608]{0:T(1024)(128)(4,1)}), s8[4194304]{0:T(1024)(128)(4,1)S(1)}, s32[]{:S(2)}) async-start(s8[8388608]{0:T(1024)(128)(4,1)} %bitcast.226), calls=%async_computation.7 | async-start | bytes 8388608
  634.2 13.6 %slice-start.5 = ((s8[8388608]{0:T(1024)(128)(4,1)}), s8[4194304]{0:T(1024)(128)(4,1)S(1)}, s32[]{:S(2)}) async-start(s8[8388608]{0:T(1024)(128)(4,1)} %bitcast.226), calls=%async_computation.8 | async-start | bytes 8388608
  647.8 18.4 %collective-permute-start.2 = (bf16[4,2,128,2,128]{2,4,3,1,0:T(8,128)(2,1)S(1)}, bf16[4,2,128,2,128]{2,4,3,1,0:T(8,128)(2,1)S(1)}, u32[]{:S(2)}, u32[]{:S(2)}) collective-permute-start(bf16[4,2,128,2,128]{2,4,3,1,0:T(8,128)(2,1)S(1)} %slice.450), channel_id=1, source_target_pairs={{29,0},{0,1},{1,4},{4,5},{5,8},{8,9},{9,12},{12,13},{13,16},{16,17... | collective-permute-start | bytes 1572872 | tf_op jit(solution)/shard_map/ppermute | solution.py:15
  677.4 3.2 copy-start.8
  680.7 15.5 %slice-start = ((s8[14680064]{0:T(1024)(128)(4,1)}), s8[4194304]{0:T(1024)(128)(4,1)S(1)}, s32[]{:S(2)}) async-start(s8[14680064]{0:T(1024)(128)(4,1)} %bitcast.224), calls=%async_computation.3 | async-start | bytes 8388608
  680.7 15.5 %slice-start.1 = ((s8[14680064]{0:T(1024)(128)(4,1)}), s8[4194304]{0:T(1024)(128)(4,1)S(1)}, s32[]{:S(2)}) async-start(s8[14680064]{0:T(1024)(128)(4,1)} %bitcast.224), calls=%async_computation.4 | async-start | bytes 8388608
  680.7 15.6 %slice-start.2 = ((s8[14680064]{0:T(1024)(128)(4,1)}), s8[2097152]{0:T(1024)(128)(4,1)S(1)}, s32[]{:S(2)}) async-start(s8[14680064]{0:T(1024)(128)(4,1)} %bitcast.224), calls=%async_computation.5 | async-start | bytes 4194304
  690.6 5.6 slice-start.3
  698.1 3.3 copy-start.10
  701.4 8.5 %collective-permute-start.3 = (bf16[4,2,128,1,128]{2,4,3,1,0:T(8,128)(2,1)S(1)}, bf16[4,2,128,1,128]{2,4,3,1,0:T(8,128)(2,1)S(1)}, u32[]{:S(2)}, u32[]{:S(2)}) collective-permute-start(bf16[4,2,128,1,128]{2,4,3,1,0:T(8,128)(2,1)S(1)} %slice.451), channel_id=1, source_target_pairs={{29,0},{0,1},{1,4},{4,5},{5,8},{8,9},{9,12},{12,13},{13,16},{16,17... | collective-permute-start | bytes 786440 | tf_op jit(solution)/shard_map/ppermute | solution.py:15
  721.4 4.9 copy-start.2
  732.0 3.4 copy-start.9
Sparse Core Ops, SparseCore 0:
  527.2 41.1 all-reduce.1
